TPU v7x, 32 devices: a whole 2x2x4 slice. The times are simulated.
32 devices in a mesh: inst: 4 (over x, core), dp: 4 (over z), tp: 2 (over y).
Axes of the slice: x: 2, y: 2, z: 4, core: 2. Of those that a mesh axis runs over, the one named last changes fastest.
Arguments:
- kernel_grads: bfloat16 [16, 2, 128, 4608], P(('inst', 'dp'), 'tp'), may hold values from -0.75 to 0.75
- kernel_master: float32 [2, 128, 4608], P('tp', 'dp'), may hold values from -6 to 6
- kernel_first: float32 [2, 128, 4608], P('tp', 'dp'), may hold values from -3 to 3
- kernel_second: float32 [2, 128, 4608], P('tp', 'dp'), may hold values from 0.05 to 4
- gain_grads: bfloat16 [32, 4, 4608], P(('inst', 'dp', 'tp')), may hold values from -0.29882812 to 0.29882812
- gain_master: float32 [4, 4608], replicated, may hold values from -6 to 6
- gain_first: float32 [4, 4608], replicated, may hold values from -3 to 3
- gain_second: float32 [4, 4608], replicated, may hold values from 0.05 to 4
Outputs:
- kernel_params: bfloat16 [2, 128, 4608], P('tp')
- kernel_master_new: float32 [2, 128, 4608], P('tp', 'dp')
- kernel_first_new: float32 [2, 128, 4608], P('tp', 'dp')
- kernel_second_new: float32 [2, 128, 4608], P('tp', 'dp')
- gain_params: bfloat16 [4, 4608], replicated
- gain_master_new: float32 [4, 4608], replicated
- gain_first_new: float32 [4, 4608], replicated
- gain_second_new: float32 [4, 4608], replicated
All inputs are finite; a program needn't handle non-finite values.
Results may differ from a plain program's by a relative error of at most 0.004.
Values may be sent and summed in bfloat16 or wider, within the bound.
A program may use at most 64 MiB of HBM per device.

v0:
```python
import jax
import jax.numpy as jnp
from jax import lax
from jax.sharding import PartitionSpec as P

beta_one = 0.9
beta_two = 0.95
learn_rate = 0.01
decay_rate = 0.1
epsilon = 1e-08
step_count = 100.0


def adam_update(gradient, master, first_moment, second_moment):
    first_next = beta_one * first_moment + (1.0 - beta_one) * gradient
    second_next = beta_two * second_moment + (1.0 - beta_two) * gradient * gradient
    first_hat = first_next / (1.0 - beta_one**step_count)
    second_hat = second_next / (1.0 - beta_two**step_count)
    master_next = master - learn_rate * (
        first_hat / (jnp.sqrt(second_hat) + epsilon) + decay_rate * master
    )
    return (master_next, first_next, second_next)


def local(
    kernel_grads,
    kernel_master,
    kernel_first,
    kernel_second,
    gain_grads,
    gain_master,
    gain_first,
    gain_second,
):
    local_grads = kernel_grads[0].astype(jnp.float32)
    gain_local = gain_grads[0].astype(jnp.float32)
    flat_grads = gain_local.reshape(-1)
    gain_whole = None
    partial_rows, gain_piece = (
        lax.psum_scatter(
            local_grads.astype(jnp.bfloat16), "dp", scatter_dimension=1, tiled=True
        ).astype(jnp.float32),
        lax.psum_scatter(
            flat_grads.astype(jnp.bfloat16), "dp", scatter_dimension=0, tiled=True
        ).astype(jnp.float32),
    )
    gradient, gain_piece = (
        lax.psum(partial_rows.astype(jnp.bfloat16), "inst").astype(jnp.float32),
        lax.psum(gain_piece.astype(jnp.bfloat16), "inst").astype(jnp.float32),
    )
    kernel_master_new, kernel_first_new, kernel_second_new = adam_update(
        gradient, kernel_master, kernel_first, kernel_second
    )
    kernel_params = lax.all_gather(kernel_master_new.astype(jnp.bfloat16), "dp", axis=1, tiled=True)
    gain_piece = lax.psum(gain_piece, "tp")
    gain_whole = lax.all_gather(gain_piece, "dp", axis=0, tiled=True).reshape(gain_master.shape)
    gain_master_new, gain_first_new, gain_second_new = adam_update(
        gain_whole, gain_master, gain_first, gain_second
    )
    gain_params = gain_master_new.astype(jnp.bfloat16)
    return (
        kernel_params,
        kernel_master_new,
        kernel_first_new,
        kernel_second_new,
        gain_params,
        gain_master_new,
        gain_first_new,
        gain_second_new,
    )


def solution(mesh):
    return jax.shard_map(
        local,
        mesh=mesh,
        in_specs=(
            P(("inst", "dp"), "tp", None, None),
            P("tp", "dp", None),
            P("tp", "dp", None),
            P("tp", "dp", None),
            P(("inst", "dp", "tp"), None, None),
            P(),
            P(),
            P(),
        ),
        out_specs=(
            P("tp", None, None),
            P("tp", "dp", None),
            P("tp", "dp", None),
            P("tp", "dp", None),
            P(),
            P(),
            P(),
            P(),
        ),
        check_vma=False,
    )
```

profile of v0, /device:TPU:0, one launch (start us, length us, event | category | flops | bytes accessed | tf_op | source)
XLA Modules:
  0.0 142.5 jit_solution(16182226304347898728)
XLA Ops:
  7.2 0.0 copy-start.1
  7.2 0.0 copy-start
  7.2 0.0 reduce-scatter.2.cloned.1.call-start
  7.2 0.7 reduce-scatter.2.cloned.1.call-update
  7.9 0.0 all-reduce.3.cloned.1.call-start
  8.0 34.4 %reduce-scatter.2.cloned.1.call-done = bf16[1,32,4608]{2,1,0:T(8,128)(2,1)} async-done(((bf16[1,128,4608]{2,1,0:T(8,128)(2,1)}), bf16[1,32,4608]{2,1,0:T(8,128)(2,1)}) %reduce-scatter.2.cloned.1.call-update) | async-done | bytes 294928 | tf_op jit(solution)/shard_map/reduce_scatter | solution.py:40
  42.4 0.0 all-reduce.3.cloned.1.call-update
  42.4 0.0 copy-start.5
  42.4 0.0 copy-start.6
  42.4 0.0 copy-start.2
  42.5 0.0 all-gather.3.cloned.1.call-start
  42.5 33.3 %all-reduce.3.cloned.1.call-done = bf16[1,32,4608]{2,1,0:T(8,128)(2,1)} async-done(((bf16[1,32,4608]{2,1,0:T(8,128)(2,1)}), bf16[1,32,4608]{2,1,0:T(8,128)(2,1)}) %all-reduce.3.cloned.1.call-update) | async-done | bytes 294928 | tf_op jit(solution)/shard_map/psum | solution.py:48
  75.8 0.0 copy-done
  75.8 2.7 %fusion.7 = (bf16[1,32,4608]{2,1,0:T(8,128)(2,1)}, f32[1,32,4608]{2,1,0:T(8,128)}, f32[1,32,4608]{2,1,0:T(8,128)}, f32[1,32,4608]{2,1,0:T(8,128)}) fusion(f32[1,32,4608]{2,1,0:T(8,128)S(1)} %copy-done, bf16[1,32,4608]{2,1,0:T(8,128)(2,1)} %all-reduce.3.cloned.1.call-done, f32[1,32,4608]{2,1,0:T(8,128)S(1)} %copy-done.1, f32[1,32,4608]{2,1,0:T(8,128)} %param.11), kind=kLoop, calls=%fused_computation.11 | loop fusion | flops 2506752 | bytes 4128768 | tf_op jit(solution)/shard_map/convert_element_type | solution.py:54
  78.5 0.0 all-gather.3.cloned.1.call-update
  78.6 0.6 dynamic-slice
  79.9 20.5 %all-reduce = bf16[18432]{0:T(1024)(128)(2,1)S(1)} all-reduce(bf16[18432]{0:T(1024)(128)(2,1)S(1)} %squeeze.7), channel_id=3, replica_groups=mesh['inst'=4,'dp'=4,'tp'=2] {'dp'}, use_global_device_ids=true, to_apply=%region_2.0.clone | all-reduce | flops 18432 | bytes 73728
  100.4 0.1 dynamic-slice.1
  100.5 10.9 %psum.22 = bf16[4608]{0:T(1024)(128)(2,1)S(1)} all-reduce(bf16[4608]{0:T(1024)(128)(2,1)S(1)} %dynamic-slice.1), channel_id=1, replica_groups=mesh['inst'=4,'dp'=4,'tp'=2] {'inst'}, use_global_device_ids=true, to_apply=%region_3.0 | all-reduce | flops 4608 | bytes 18432 | tf_op jit(solution)/shard_map/psum | solution.py:49
  111.4 8.2 %psum.23 = f32[4608]{0:T(1024)S(1)} all-reduce(bf16[4608]{0:T(1024)(128)(2,1)S(1)} %psum.22), channel_id=1, replica_groups=mesh['inst'=4,'dp'=4,'tp'=2] {'tp'}, use_global_device_ids=true, to_apply=%region_4.0 | all-reduce | flops 4608 | bytes 27648 | tf_op jit(solution)/shard_map/psum | solution.py:55
  119.6 13.2 %all-gather = f32[4,1,4608]{2,1,0:T(1,128)S(1)} all-gather(f32[1,1,4608]{2,1,0:T(1,128)S(1)} %reshape.22), channel_id=1, replica_groups=mesh['inst'=4,'dp'=4,'tp'=2] {'dp'}, dimensions={0}, use_global_device_ids=true | all-gather | bytes 92160 | tf_op jit(solution)/shard_map/all_gather | solution.py:56
  132.8 0.0 copy-done.4
  132.8 0.8 fusion.4
  133.6 2.4 %copy.23 = bf16[1,128,4608]{2,1,0:T(8,128)(2,1)} copy(bf16[1,128,4608]{2,1,0:T(8,128)(2,1)} %all-gather.3.cloned.1.call-done) | data formatting | bytes 2359296
  (10 shorter events, 0.0 us)
Async XLA Ops:
  7.2 68.6 %copy-start.1 = (f32[1,32,4608]{2,1,0:T(8,128)S(1)}, f32[1,32,4608]{2,1,0:T(8,128)}, u32[]{:S(2)}) copy-start(f32[1,32,4608]{2,1,0:T(8,128)} %param.10) | copy-start | bytes 1769476
  7.2 68.6 %copy-start = (f32[1,32,4608]{2,1,0:T(8,128)S(1)}, f32[1,32,4608]{2,1,0:T(8,128)}, u32[]{:S(2)}) copy-start(f32[1,32,4608]{2,1,0:T(8,128)} %param.9) | copy-start | bytes 1769476
  7.2 35.2 %reduce-scatter.2.cloned.1.call-start = ((), (), s32[]{:S(2)}) async-start(), calls=%async_computation.1 | async-start | bytes 1474560 | tf_op jit(solution)/shard_map/reduce_scatter | solution.py:40
  7.9 67.9 %all-reduce.3.cloned.1.call-start = ((), (), s32[]{:S(2)}) async-start(), calls=%async_computation.2 | async-start | bytes 589824 | tf_op jit(solution)/shard_map/psum | solution.py:48
  42.4 36.2 %copy-start.5 = (bf16[1,4,4608]{2,1,0:T(4,128)(2,1)S(1)}, bf16[1,4,4608]{2,1,0:T(4,128)(2,1)}, u32[]{:S(2)}) copy-start(bf16[1,4,4608]{2,1,0:T(4,128)(2,1)} %param.12) | copy-start | bytes 110596
  42.4 36.2 %copy-start.6 = (u32[32]{0:T(128)S(1)}, u32[32]{0:T(128)}, u32[]{:S(2)}) copy-start(u32[32]{0:T(128)} %constant.35) | copy-start | bytes 388
  42.4 90.3 %copy-start.2 = (f32[4,4608]{1,0:T(4,128)S(1)}, f32[4,4608]{1,0:T(4,128)}, u32[]{:S(2)}) copy-start(f32[4,4608]{1,0:T(4,128)} %param.13) | copy-start | bytes 221188
  42.4 90.3 %copy-start.3 = (f32[4,4608]{1,0:T(4,128)S(1)}, f32[4,4608]{1,0:T(4,128)}, u32[]{:S(2)}) copy-start(f32[4,4608]{1,0:T(4,128)} %param.14) | copy-start | bytes 221188
  42.5 90.3 %copy-start.4 = (f32[4,4608]{1,0:T(4,128)S(1)}, f32[4,4608]{1,0:T(4,128)}, u32[]{:S(2)}) copy-start(f32[4,4608]{1,0:T(4,128)} %param.15) | copy-start | bytes 221188
  42.5 91.1 %all-gather.3.cloned.1.call-start = ((), (), s32[]{:S(2)}) async-start(), calls=%async_computation.3 | async-start | bytes 1474560 | tf_op jit(solution)/shard_map/all_gather | solution.py:54
Sparse Core Ops, SparseCore 0:
  10.3 32.0 reduce-scatter.1
  44.7 31.0 all-reduce.2
  78.7 30.9 all-gather.2
where the time goes:
time: 143 us; the launch traced here: 142 us
  waiting for transfers between devices  68.4 us (48%)
  blocking collectives  52.8 us (37%)
  between operations  14.5 us (10%)
  other arithmetic  3.55 us (2%)
  local copies, waits for them, and re-layouts  3.1 us (2%)
    reduce_scatter x1, waiting for transfers between devices, local(): lax.psum_scatter(local_grads.astype(jnp.bfloat16), 'dp', scatter_dimensio...  34.4 us
    psum x1, waiting for transfers between devices, local(): lax.psum(partial_rows.astype(jnp.bfloat16), 'inst').astype(jnp.float32)  33.3 us
    unnamed x1, blocking collectives  20.5 us
    all_gather x1, blocking collectives, local(): lax.all_gather(gain_piece, 'dp', axis=0, tiled=True)  13.2 us
    psum x1, blocking collectives, local(): lax.psum(gain_piece.astype(jnp.bfloat16), 'inst').astype(jnp.float32)  10.9 us
    psum x1, blocking collectives, local(): gain_piece = lax.psum(gain_piece, 'tp')  8.21 us
    unnamed x18, local copies, waits for them, and re-layouts  3.08 us
  transfers between devices with their start and end apart: 3, of which 2 were waited for; matrix products, arithmetic and copies ran while one was open for 1% of the time, Pallas kernels for 0%

commit v1 on v0

--- a/solution.py
+++ b/solution.py
@@ -2,6 +2,7 @@
 import jax.numpy as jnp
 from jax import lax
 from jax.sharding import PartitionSpec as P
+from jax.lax import all_to_all, psum
 
 beta_one = 0.9
 beta_two = 0.95
@@ -53,7 +54,14 @@
     )
     kernel_params = lax.all_gather(kernel_master_new.astype(jnp.bfloat16), "dp", axis=1, tiled=True)
     gain_piece = lax.psum(gain_piece, "tp")
-    gain_whole = lax.all_gather(gain_piece, "dp", axis=0, tiled=True).reshape(gain_master.shape)
+
+    def part_rings_now(block_in, comm_axis):
+        front = psum(1, axis_name=comm_axis)
+        res = jnp.stack(front * [block_in], axis=0)
+        lower = all_to_all(res, axis_name=comm_axis, split_axis=0, concat_axis=0)
+        return jnp.concatenate(lower, axis=0)
+
+    gain_whole = part_rings_now(gain_piece, comm_axis="dp").reshape(gain_master.shape)
     gain_master_new, gain_first_new, gain_second_new = adam_update(
         gain_whole, gain_master, gain_first, gain_second
     )

time: 143 us -> 138 us (0.965)
  blocking collectives: 52.8 us -> 47.8 us
    all_gather x1 -> x0, blocking collectives: 13.2 us -> none  [local(): lax.all_gather(gain_piece, 'dp', axis=0, tiled=True)]
    all_to_all x0 -> x1, blocking collectives: none -> 8.13 us  [part_rings_now(): lower = all_to_all(res, axis_name=comm_axis, split_axis=0, concat_axis=0)]
    unnamed x18 -> x17, local copies, waits for them, and re-layouts: 3.08 us -> 3.06 us
where the time goes in v1:
time: 138 us; the launch traced here: 137 us
  waiting for transfers between devices  68.4 us (50%)
  blocking collectives  47.8 us (35%)
  between operations  14.5 us (11%)
  other arithmetic  3.55 us (3%)
  local copies, waits for them, and re-layouts  3.12 us (2%)
    reduce_scatter x1, waiting for transfers between devices, local(): lax.psum_scatter(local_grads.astype(jnp.bfloat16), 'dp', scatter_dimensio...  34.4 us
    psum x1, waiting for transfers between devices, local(): lax.psum(partial_rows.astype(jnp.bfloat16), 'inst').astype(jnp.float32)  33.3 us
    unnamed x1, blocking collectives  20.5 us
    psum x1, blocking collectives, local(): lax.psum(gain_piece.astype(jnp.bfloat16), 'inst').astype(jnp.float32)  10.9 us
    psum x1, blocking collectives, local(): gain_piece = lax.psum(gain_piece, 'tp')  8.21 us
    all_to_all x1, blocking collectives, part_rings_now(): lower = all_to_all(res, axis_name=comm_axis, split_axis=0, concat_axis=0)  8.13 us
    unnamed x17, local copies, waits for them, and re-layouts  3.06 us
  transfers between devices with their start and end apart: 3, of which 2 were waited for; matrix products, arithmetic and copies ran while one was open for 1% of the time, Pallas kernels for 0%

profile of v1, /device:TPU:0, one launch (start us, length us, event | category | flops | bytes accessed | tf_op | source)
XLA Modules:
  0.0 137.5 jit_solution(16669459855133718223)
XLA Ops:
  7.2 0.0 copy-start.1
  7.2 0.0 copy-start
  7.2 0.0 reduce-scatter.2.cloned.1.call-start
  7.2 0.7 reduce-scatter.2.cloned.1.call-update
  7.9 0.0 all-reduce.3.cloned.1.call-start
  8.0 34.4 %reduce-scatter.2.cloned.1.call-done = bf16[1,32,4608]{2,1,0:T(8,128)(2,1)} async-done(((bf16[1,128,4608]{2,1,0:T(8,128)(2,1)}), bf16[1,32,4608]{2,1,0:T(8,128)(2,1)}) %reduce-scatter.2.cloned.1.call-update) | async-done | bytes 294928 | tf_op jit(solution)/shard_map/reduce_scatter | solution.py:41
  42.4 0.0 all-reduce.3.cloned.1.call-update
  42.4 0.0 copy-start.5
  42.4 0.0 copy-start.6
  42.5 0.0 all-gather.2.cloned.1.call-start
  42.5 33.3 %all-reduce.3.cloned.1.call-done = bf16[1,32,4608]{2,1,0:T(8,128)(2,1)} async-done(((bf16[1,32,4608]{2,1,0:T(8,128)(2,1)}), bf16[1,32,4608]{2,1,0:T(8,128)(2,1)}) %all-reduce.3.cloned.1.call-update) | async-done | bytes 294928 | tf_op jit(solution)/shard_map/psum | solution.py:49
  75.8 0.0 copy-done
  75.8 2.7 %fusion.7 = (bf16[1,32,4608]{2,1,0:T(8,128)(2,1)}, f32[1,32,4608]{2,1,0:T(8,128)}, f32[1,32,4608]{2,1,0:T(8,128)}, f32[1,32,4608]{2,1,0:T(8,128)}) fusion(f32[1,32,4608]{2,1,0:T(8,128)S(1)} %copy-done, bf16[1,32,4608]{2,1,0:T(8,128)(2,1)} %all-reduce.3.cloned.1.call-done, f32[1,32,4608]{2,1,0:T(8,128)S(1)} %copy-done.1, f32[1,32,4608]{2,1,0:T(8,128)} %param.11), kind=kLoop, calls=%fused_computation.11 | loop fusion | flops 2506752 | bytes 4128768 | tf_op jit(solution)/shard_map/convert_element_type | solution.py:55
  78.5 0.0 all-gather.2.cloned.1.call-update
  78.6 0.6 dynamic-slice
  79.9 20.5 %all-reduce = bf16[18432]{0:T(1024)(128)(2,1)S(1)} all-reduce(bf16[18432]{0:T(1024)(128)(2,1)S(1)} %squeeze.7), channel_id=3, replica_groups=mesh['inst'=4,'dp'=4,'tp'=2] {'dp'}, use_global_device_ids=true, to_apply=%region_2.0.clone | all-reduce | flops 18432 | bytes 73728
  100.4 0.1 dynamic-slice.1
  100.5 10.9 %psum.22 = bf16[4608]{0:T(1024)(128)(2,1)S(1)} all-reduce(bf16[4608]{0:T(1024)(128)(2,1)S(1)} %dynamic-slice.1), channel_id=1, replica_groups=mesh['inst'=4,'dp'=4,'tp'=2] {'inst'}, use_global_device_ids=true, to_apply=%region_3.0 | all-reduce | flops 4608 | bytes 18432 | tf_op jit(solution)/shard_map/psum | solution.py:50
  111.4 8.2 %psum.23 = f32[4608]{0:T(1024)S(1)} all-reduce(bf16[4608]{0:T(1024)(128)(2,1)S(1)} %psum.22), channel_id=1, replica_groups=mesh['inst'=4,'dp'=4,'tp'=2] {'tp'}, use_global_device_ids=true, to_apply=%region_4.0 | all-reduce | flops 4608 | bytes 27648 | tf_op jit(solution)/shard_map/psum | solution.py:56
  119.6 8.1 %all_to_all.9 = f32[4,1,4608]{2,1,0:T(1,128)S(1)} all-to-all(f32[4,1,4608]{2,1,0:T(1,128)S(1)} %stack.2), channel_id=1, replica_groups=mesh['inst'=4,'dp'=4,'tp'=2] {'dp'}, dimensions={0} | all-to-all | bytes 147456 | tf_op jit(solution)/shard_map/all_to_all | solution.py:61
  127.8 0.0 copy-done.2
  127.8 0.0 copy-done.4
  127.8 0.8 fusion.4
  128.6 2.4 %copy.23 = bf16[1,128,4608]{2,1,0:T(8,128)(2,1)} copy(bf16[1,128,4608]{2,1,0:T(8,128)(2,1)} %all-gather.2.cloned.1.call-done) | data formatting | bytes 2359296
  (10 shorter events, 0.1 us)
Async XLA Ops:
  7.2 68.6 %copy-start.1 = (f32[1,32,4608]{2,1,0:T(8,128)S(1)}, f32[1,32,4608]{2,1,0:T(8,128)}, u32[]{:S(2)}) copy-start(f32[1,32,4608]{2,1,0:T(8,128)} %param.10) | copy-start | bytes 1769476
  7.2 68.6 %copy-start = (f32[1,32,4608]{2,1,0:T(8,128)S(1)}, f32[1,32,4608]{2,1,0:T(8,128)}, u32[]{:S(2)}) copy-start(f32[1,32,4608]{2,1,0:T(8,128)} %param.9) | copy-start | bytes 1769476
  7.2 35.2 %reduce-scatter.2.cloned.1.call-start = ((), (), s32[]{:S(2)}) async-start(), calls=%async_computation.2 | async-start | bytes 1474560 | tf_op jit(solution)/shard_map/reduce_scatter | solution.py:41
  7.9 67.9 %all-reduce.3.cloned.1.call-start = ((), (), s32[]{:S(2)}) async-start(), calls=%async_computation.3 | async-start | bytes 589824 | tf_op jit(solution)/shard_map/psum | solution.py:49
  42.4 36.2 %copy-start.5 = (bf16[1,4,4608]{2,1,0:T(4,128)(2,1)S(1)}, bf16[1,4,4608]{2,1,0:T(4,128)(2,1)}, u32[]{:S(2)}) copy-start(bf16[1,4,4608]{2,1,0:T(4,128)(2,1)} %param.12) | copy-start | bytes 110596
  42.4 36.2 %copy-start.6 = (u32[32]{0:T(128)S(1)}, u32[32]{0:T(128)}, u32[]{:S(2)}) copy-start(u32[32]{0:T(128)} %constant.35) | copy-start | bytes 388
  42.4 85.3 %copy-start.2 = (f32[4,4608]{1,0:T(4,128)S(1)}, f32[4,4608]{1,0:T(4,128)}, u32[]{:S(2)}) copy-start(f32[4,4608]{1,0:T(4,128)} %param.13) | copy-start | bytes 221188
  42.4 85.3 %copy-start.3 = (f32[4,4608]{1,0:T(4,128)S(1)}, f32[4,4608]{1,0:T(4,128)}, u32[]{:S(2)}) copy-start(f32[4,4608]{1,0:T(4,128)} %param.14) | copy-start | bytes 221188
  42.5 85.3 %copy-start.4 = (f32[4,4608]{1,0:T(4,128)S(1)}, f32[4,4608]{1,0:T(4,128)}, u32[]{:S(2)}) copy-start(f32[4,4608]{1,0:T(4,128)} %param.15) | copy-start | bytes 221188
  42.5 86.1 %all-gather.2.cloned.1.call-start = ((), (), s32[]{:S(2)}) async-start(), calls=%async_computation.4 | async-start | bytes 1474560 | tf_op jit(solution)/shard_map/all_gather | solution.py:55
Sparse Core Ops, SparseCore 0:
  10.3 32.0 reduce-scatter.1
  44.7 31.0 all-reduce.2
  78.7 30.9 all-gather.1
